TPU v7x, 32 devices: a whole 2x2x4 slice. The times are simulated.
32 devices in a mesh: member: 4 (over z), lat: 4 (over y, core), lon: 2 (over x).
Axes of the slice: x: 2, y: 2, z: 4, core: 2. Of those that a mesh axis runs over, the one named last changes fastest.
Arguments:
- state: bfloat16 [100, 8, 720], P(None, 'lat', 'lon'), may hold values from -6 to 6
- target: bfloat16 [100, 8, 720], P(None, 'lat', 'lon'), may hold values from -6 to 6
- land_sea: int32 [8, 720], P('lat', 'lon'), may hold values 0 or 1
- seeds: int32 [4, 32], P('member'), may hold values from 0 to 65535
- w_in: bfloat16 [9, 100, 256], replicated, may hold values from -0.1875 to 0.1875
- w_mid: bfloat16 [9, 256, 256], replicated, may hold values from -0.125 to 0.125
- w_out: bfloat16 [100, 256], replicated, may hold values from -0.375 to 0.375
- w_noise: float32 [32, 256], replicated, may hold values from -1 to 1
Outputs:
- update_in: float32 [9, 100, 256], replicated
- update_mid: float32 [9, 256, 256], replicated
- update_out: float32 [100, 256], replicated
- update_noise: float32 [32, 256], replicated
- loss: float32 [], replicated
All inputs are finite; a program needn't handle non-finite values. No bound on the sum of `land_sea` on one device may be relied on, other than what follows from the above.
Results may differ from a plain program's by a relative error of at most 0.0014.
Values may be sent and summed in bfloat16 or wider, within the bound.
A program may use at most 64 MiB of HBM per device.

v0:
```python
import jax
import jax.numpy as jnp
from jax import lax
from jax.sharding import PartitionSpec as P

SMOOTH = 0.25


def with_halo(block, sides, width):
    for axis, dim in sides:
        count = lax.axis_size(axis)
        forward = [(i, i + 1) for i in range(count - 1)]
        forward.append((count - 1, 0))
        backward = [(target, source) for source, target in forward]
        low = lax.ppermute(
            lax.slice_in_dim(block, block.shape[dim] - width, None, axis=dim), axis, forward
        )
        high = lax.ppermute(lax.slice_in_dim(block, 0, width, axis=dim), axis, backward)
        block = jnp.concatenate([low, block, high], axis=dim)
    return block


def shifted(padded, offset, row_count, col_count):
    row_shift = offset // 3
    col_shift = offset % 3
    window = padded[:, row_shift : row_shift + row_count, col_shift : col_shift + col_count]
    return window.reshape(padded.shape[0], row_count * col_count)


def conv_forward(weights, padded, row_count, col_count):
    summed = None
    for offset in range(9):
        window = shifted(padded, offset, row_count, col_count)
        part = lax.dot_general(
            weights[offset], window, (((0,), (0,)), ((), ())), preferred_element_type=jnp.float32
        )
        summed = part if summed is None else summed + part
    return summed


def conv_back(weights, padded, row_count, col_count):
    summed = None
    for offset in range(9):
        window = shifted(padded, 8 - offset, row_count, col_count)
        part = jnp.dot(weights[offset], window, preferred_element_type=jnp.float32)
        summed = part if summed is None else summed + part
    return summed


def weight_grad(padded, deltas, row_count, col_count):
    parts = []
    for offset in range(9):
        window = shifted(padded, offset, row_count, col_count)
        parts.append(
            lax.dot_general(
                window, deltas, (((1,), (1,)), ((), ())), preferred_element_type=jnp.float32
            )
        )
    return jnp.stack(parts)


def gelu_pair(pre):
    return jax.jvp(jax.nn.gelu, (pre,), (jnp.ones_like(pre),))


def clear_outside(padded, width, lat_index, lat_count):
    row_count = padded.shape[1] - 2 * width
    global_row = lat_index * row_count + jnp.arange(padded.shape[1], dtype=jnp.int32) - width
    inside = (global_row >= 0) & (global_row < row_count * lat_count)
    return jnp.where(inside[None, :, None], padded, jnp.zeros((), padded.dtype))


def combine(outputs, target_flat, weights, slope_sum, spread_sum, members):
    misses = outputs - target_flat[None]
    radius = jnp.sqrt(misses * misses + SMOOTH * SMOOTH)
    gradients = weights[None] * (misses / radius / members - slope_sum / (members * (members - 1)))
    loss_term = jnp.sum(
        weights[None] * ((radius - SMOOTH) / members - spread_sum / (2 * members * (members - 1)))
    )
    return (gradients, loss_term)


def pair_sums(outputs, others, running):

    def add_member(totals, member_out):
        gap_value = outputs - member_out.astype(jnp.float32)[None]
        radius = jnp.sqrt(gap_value * gap_value + SMOOTH * SMOOTH)
        return ((totals[0] + gap_value / radius, totals[1] + radius - SMOOTH), None)

    sums, _ = lax.scan(add_member, running, others)
    return sums


def normalize(gradient):
    return gradient / jnp.sqrt(jnp.mean(gradient * gradient) + 1e-06)


def body(state, target, land_sea, seeds, w_in, w_mid, w_out, w_noise):
    variables, row_count, col_count = state.shape
    channels = w_in.shape[2]
    cell_count = row_count * col_count
    lat_index = lax.axis_index("lat")
    lat_count = lax.axis_size("lat")
    members = lax.axis_size("member")
    latent = (seeds[0].astype(jnp.float32) - 32767.5) / 18918.0
    noise_bias = jnp.dot(latent, w_noise, precision=lax.Precision.HIGHEST)
    state_pad = with_halo(state, (("lat", 1), ("lon", 2)), 1)
    state_pad = clear_outside(state_pad, 1, lat_index, lat_count)
    pre_in = conv_forward(w_in, state_pad, row_count, col_count) + noise_bias[:, None]
    act_in, slope_in = gelu_pair(pre_in)
    hidden_in = act_in.astype(jnp.bfloat16)
    hidden_pad = with_halo(
        hidden_in.reshape(channels, row_count, col_count), (("lat", 1), ("lon", 2)), 1
    )
    hidden_pad = clear_outside(hidden_pad, 1, lat_index, lat_count)
    pre_mid = conv_forward(w_mid, hidden_pad, row_count, col_count)
    act_mid, slope_mid = gelu_pair(pre_mid)
    hidden_out = (act_mid + hidden_in.astype(jnp.float32)).astype(jnp.bfloat16)
    flat_state = state.reshape(variables, cell_count).astype(jnp.float32)
    output = (flat_state + jnp.dot(w_out, hidden_out, preferred_element_type=jnp.float32)).astype(
        jnp.bfloat16
    )
    target_flat = target.reshape(variables, cell_count).astype(jnp.float32)
    weights = 1.0 + land_sea.reshape(1, cell_count).astype(jnp.float32)
    own_output = output.astype(jnp.float32)[None]
    blank = jnp.zeros(own_output.shape, jnp.float32)
    slope_sum, spread_sum = pair_sums(
        own_output, lax.all_gather(output[None], "member", axis=0, tiled=True), (blank, blank)
    )
    gradients, loss_term = combine(own_output, target_flat, weights, slope_sum, spread_sum, members)
    delta_out = gradients[0].astype(jnp.bfloat16)
    grad_out = lax.dot_general(
        delta_out, hidden_out, (((1,), (1,)), ((), ())), preferred_element_type=jnp.float32
    )
    upstream = lax.dot_general(
        w_out, delta_out, (((0,), (0,)), ((), ())), preferred_element_type=jnp.float32
    )
    delta_mid = (upstream * slope_mid).astype(jnp.bfloat16)
    delta_pad = with_halo(
        delta_mid.reshape(channels, row_count, col_count), (("lat", 1), ("lon", 2)), 1
    )
    delta_pad = clear_outside(delta_pad, 1, lat_index, lat_count)
    incoming = conv_back(w_mid, delta_pad, row_count, col_count) + upstream
    delta_in = (incoming * slope_in).astype(jnp.bfloat16)
    grad_mid = weight_grad(hidden_pad, delta_mid, row_count, col_count)
    grad_in = weight_grad(state_pad, delta_in, row_count, col_count)
    grad_noise = latent[:, None] * jnp.sum(delta_in.astype(jnp.float32), axis=1)[None, :]
    grad_in, grad_mid, grad_out, grad_noise, summed = lax.psum(
        (grad_in, grad_mid, grad_out, grad_noise, loss_term), ("member", "lat", "lon")
    )
    loss = summed / (variables * cell_count * lat_count * lax.axis_size("lon"))
    return (
        normalize(grad_in),
        normalize(grad_mid),
        normalize(grad_out),
        normalize(grad_noise),
        loss,
    )


def solution(mesh):
    placed = (
        P(None, "lat", "lon"),
        P(None, "lat", "lon"),
        P("lat", "lon"),
        P("member", None),
        P(),
        P(),
        P(),
        P(),
    )
    return jax.shard_map(
        body, mesh=mesh, in_specs=placed, out_specs=(P(), P(), P(), P(), P()), check_vma=False
    )
```

profile of v0, /device:TPU:0, one launch (start us, length us, event | category | flops | bytes accessed | tf_op | source)
XLA Modules:
  0.0 255.6 jit_solution(3920980561953618674)
XLA Ops:
  7.2 1.3 fusion.124
  8.5 2.5 collective-permute-start.1
  11.9 3.4 %collective-permute-done.1 = bf16[100,1,360]{2,1,0:T(2,128)(2,1)S(1)} collective-permute-done((bf16[100,1,360]{2,1,0:T(2,128)(2,1)S(1)}, bf16[100,1,360]{2,1,0:T(2,128)(2,1)S(1)}, u32[]{:S(2)}, u32[]{:S(2)}) %collective-permute-start.1) | collective-permute-done | bytes 72032 | tf_op jit(solution)/shard_map/ppermute | solution.py:18
  16.4 1.3 pad_maximum_fusion.2
  17.7 1.6 collective-permute-start.3
  19.8 3.2 %collective-permute-done.3 = bf16[100,4,1]{2,1,0:T(4,128)(2,1)S(1)} collective-permute-done((bf16[100,4,1]{2,1,0:T(4,128)(2,1)S(1)}, bf16[100,4,1]{2,1,0:T(4,128)(2,1)S(1)}, u32[]{:S(2)}, u32[]{:S(2)}) %collective-permute-start.3) | collective-permute-done | bytes 832 | tf_op jit(solution)/shard_map/ppermute | solution.py:18
  23.0 1.1 collective-permute-done.2
  24.1 2.2 maximum_select_fusion.2
  26.3 1.4 fusion.123
  31.7 1.3 multiply_convert_fusion
  34.1 4.3 %collective-permute-done.5 = bf16[256,1,360]{0,2,1:T(8,128)(2,1)S(1)} collective-permute-done((bf16[256,1,360]{0,2,1:T(8,128)(2,1)S(1)}, bf16[256,1,360]{0,2,1:T(8,128)(2,1)S(1)}, u32[]{:S(2)}, u32[]{:S(2)}) %collective-permute-start.5) | collective-permute-done | bytes 184352 | tf_op jit(solution)/shard_map/ppermute | solution.py:18
  38.4 2.3 collective-permute-done.4
  40.8 1.6 collective-permute-start.7
  44.7 1.3 collective-permute-done.6
  49.8 1.3 add_convert_fusion
  51.4 16.8 %all-gather.1 = bf16[4,100,720]{2,1,0:T(8,128)(2,1)} all-gather(bf16[1,100,720]{2,1,0:T(8,128)(2,1)S(1)} %bitcast.306), channel_id=2, replica_groups=mesh['member'=4,'lat'=4,'lon'=2] {'member'}, dimensions={0}, use_global_device_ids=true | all-gather | bytes 720000 | tf_op jit(solution)/shard_map/all_gather | solution.py:128
  68.2 4.7 %while.15 = (s32[]{:T(128)}, f32[1,100,720]{2,1,0:T(8,128)S(1)}, f32[1,100,720]{2,1,0:T(8,128)S(1)}, bf16[4,100,720]{2,1,0:T(8,128)(2,1)}, f32[1,100,720]{2,1,0:T(8,128)S(1)}, /*index=5*/s32[]{:T(128)}, s32[]{:T(128)}) while((s32[]{:T(128)}, f32[1,100,720]{2,1,0:T(8,128)S(1)}, f32[1,100,720]{2,1,0:T(8,128)S(1)}, ...), condition=%wide.region_1.2_spmd.clone, body=%wide.region_0.1_spmd.clone.sunk | while | flops 720003 | bytes 1584099 | solution.py:90
  68.2 1.2 fusion.194
  69.4 1.2 fusion.194
  70.6 1.2 fusion.194
  71.7 1.2 fusion.194
  72.9 1.8 fusion.51
  74.8 1.7 fusion.49
  80.2 1.1 collective-permute-done.9
  81.2 2.4 collective-permute-done.8
  83.8 2.0 collective-permute-start.10
  95.2 40.8 %all-reduce = (f32[32,256]{1,0:T(8,128)S(1)}, f32[]{:T(128)}) all-reduce(f32[32,256]{1,0:T(8,128)S(1)} %broadcast_multiply_fusion, f32[]{:T(128)} %get-tuple-element.130), channel_id=1, replica_groups=mesh['member'=4,'lat'=4,'lon'=2] {'member','lat','lon'}, use_global_device_ids=true, to_apply=%region_9.10 | all-reduce | flops 8193 | bytes 65544 | tf_op jit(solution)/shard_map/psum | solution.py:148
  138.6 98.4 %all-reduce.4.cloned.1.call-done = (f32[9,100,256]{2,1,0:T(8,128)}, f32[9,256,256]{2,1,0:T(8,128)}, f32[100,256]{1,0:T(8,128)}) async-done(((f32[9,100,256]{2,1,0:T(8,128)}, f32[9,256,256]{2,1,0:T(8,128)}, f32[100,256]{1,0:T(8,128)}), (f32[9,100,256]{2,1,0:T(8,128)}, f32[9,256,256]{2,1,0:T(8,128)}, f32[100,256]{1,0:T(8,128)})) %all-reduce.4.cloned.1.call-update) | async-done | bytes 3383312 | tf_op jit(solution)/shard_map/psum | solution.py:148
  237.0 2.2 multiply_reduce_fusion.1
  239.9 2.2 broadcast_divide_fusion.1
  242.1 1.2 multiply_reduce_fusion
  244.0 1.6 broadcast_divide_fusion
  (181 shorter events, 28.9 us)
Async XLA Ops:
  7.2 43.9 %copy-start = (bf16[100,256]{1,0:T(8,128)(2,1)S(1)}, bf16[100,256]{1,0:T(8,128)(2,1)}, u32[]{:S(2)}) copy-start(bf16[100,256]{1,0:T(8,128)(2,1)} %param.16) | copy-start | bytes 153604
  7.2 229.8 %all-reduce.4.cloned.1.call-start = ((), (), s32[]{:S(2)}) async-start(), calls=%async_computation | async-start | bytes 6848512 | tf_op jit(solution)/shard_map/psum | solution.py:148
  8.5 6.8 %collective-permute-start.1 = (bf16[100,1,360]{2,1,0:T(2,128)(2,1)S(1)}, bf16[100,1,360]{2,1,0:T(2,128)(2,1)S(1)}, u32[]{:S(2)}, u32[]{:S(2)}) collective-permute-start(bf16[100,1,360]{2,1,0:T(2,128)(2,1)S(1)} %get-tuple-element.148), channel_id=1, source_target_pairs={{2,0},{4,2},{6,4},{0,6},{3,1},{5,3},{7,5},{1,7},{10,8},{12,10},{14... | collective-permute-start | bytes 216008 | tf_op jit(solution)/shard_map/ppermute | solution.py:18
  11.0 5.4 %collective-permute-start = (bf16[100,1,360]{2,1,0:T(2,128)(2,1)S(1)}, bf16[100,1,360]{2,1,0:T(2,128)(2,1)S(1)}, u32[]{:S(2)}, u32[]{:S(2)}) collective-permute-start(bf16[100,1,360]{2,1,0:T(2,128)(2,1)S(1)} %get-tuple-element.147), channel_id=1, source_target_pairs={{0,2},{2,4},{4,6},{6,0},{1,3},{3,5},{5,7},{7,1},{8,10},{10,12},{12... | collective-permute-start | bytes 216008 | tf_op jit(solution)/shard_map/ppermute | solution.py:15
  17.7 5.3 %collective-permute-start.3 = (bf16[100,4,1]{2,1,0:T(4,128)(2,1)S(1)}, bf16[100,4,1]{2,1,0:T(4,128)(2,1)S(1)}, u32[]{:S(2)}, u32[]{:S(2)}) collective-permute-start(bf16[100,4,1]{2,1,0:T(4,128)(2,1)S(1)} %get-tuple-element.133), channel_id=1, source_target_pairs={{1,0},{0,1},{3,2},{2,3},{5,4},{4,5},{7,6},{6,7},{9,8},{8,9},{11,10... | collective-permute-start | bytes 2408 | tf_op jit(solution)/shard_map/ppermute | solution.py:18
  19.2 4.8 %collective-permute-start.2 = (bf16[100,4,1]{2,1,0:T(4,128)(2,1)S(1)}, bf16[100,4,1]{2,1,0:T(4,128)(2,1)S(1)}, u32[]{:S(2)}, u32[]{:S(2)}) collective-permute-start(bf16[100,4,1]{2,1,0:T(4,128)(2,1)S(1)} %get-tuple-element.132), channel_id=1, source_target_pairs={{0,1},{1,0},{2,3},{3,2},{4,5},{5,4},{6,7},{7,6},{8,9},{9,8},{10,11... | collective-permute-start | bytes 2408 | tf_op jit(solution)/shard_map/ppermute | solution.py:15
  27.9 1.6 copy-start.33
  28.4 1.8 copy-start.27
  28.6 1.9 copy-start.25
  28.7 2.0 copy-start.23
  28.9 2.2 copy-start.21
  29.1 2.3 copy-start.19
  29.2 2.4 copy-start.37
  31.7 11.2 %copy-start.42 = (s32[2,360]{1,0:T(2,128)S(1)}, s32[2,360]{1,0:T(2,128)}, u32[]{:S(2)}) copy-start(s32[2,360]{1,0:T(2,128)} %param.12) | copy-start | bytes 8644
  31.7 11.2 %copy-start.2 = (bf16[100,2,360]{2,1,0:T(2,128)(2,1)S(1)}, bf16[100,2,360]{2,1,0:T(2,128)(2,1)}, u32[]{:S(2)}) copy-start(bf16[100,2,360]{2,1,0:T(2,128)(2,1)} %param.10) | copy-start | bytes 432004
  33.0 10.7 %copy-start.41 = (bf16[100,2,360]{2,1,0:T(2,128)(2,1)S(1)}, bf16[100,2,360]{2,1,0:T(2,128)(2,1)}, u32[]{:S(2)}) copy-start(bf16[100,2,360]{2,1,0:T(2,128)(2,1)} %param.11) | copy-start | bytes 432004
  33.0 5.4 %collective-permute-start.5 = (bf16[256,1,360]{0,2,1:T(8,128)(2,1)S(1)}, bf16[256,1,360]{0,2,1:T(8,128)(2,1)S(1)}, u32[]{:S(2)}, u32[]{:S(2)}) collective-permute-start(bf16[256,1,360]{0,2,1:T(8,128)(2,1)S(1)} %get-tuple-element.137), channel_id=1, source_target_pairs={{2,0},{4,2},{6,4},{0,6},{3,1},{5,3},{7,5},{1,7},{10,8},{12,10},{14... | collective-permute-start | bytes 552968 | tf_op jit(solution)/shard_map/ppermute | solution.py:18
  34.1 6.7 %collective-permute-start.4 = (bf16[256,1,360]{0,2,1:T(8,128)(2,1)S(1)}, bf16[256,1,360]{0,2,1:T(8,128)(2,1)S(1)}, u32[]{:S(2)}, u32[]{:S(2)}) collective-permute-start(bf16[256,1,360]{0,2,1:T(8,128)(2,1)S(1)} %get-tuple-element.136), channel_id=1, source_target_pairs={{0,2},{2,4},{4,6},{6,0},{1,3},{3,5},{5,7},{7,1},{8,10},{10,12},{12... | collective-permute-start | bytes 552968 | tf_op jit(solution)/shard_map/ppermute | solution.py:15
  40.8 3.9 %collective-permute-start.7 = (bf16[256,4,1]{0,2,1:T(2,128)(2,1)S(1)}, bf16[256,4,1]{0,2,1:T(2,128)(2,1)S(1)}, u32[]{:S(2)}, u32[]{:S(2)}) collective-permute-start(bf16[256,4,1]{0,2,1:T(2,128)(2,1)S(1)} %get-tuple-element.129), channel_id=1, source_target_pairs={{1,0},{0,1},{3,2},{2,3},{5,4},{4,5},{7,6},{6,7},{9,8},{8,9},{11,10... | collective-permute-start | bytes 6152 | tf_op jit(solution)/shard_map/ppermute | solution.py:18
  42.3 3.6 %collective-permute-start.6 = (bf16[256,4,1]{0,2,1:T(2,128)(2,1)S(1)}, bf16[256,4,1]{0,2,1:T(2,128)(2,1)S(1)}, u32[]{:S(2)}, u32[]{:S(2)}) collective-permute-start(bf16[256,4,1]{0,2,1:T(2,128)(2,1)S(1)} %get-tuple-element.128), channel_id=1, source_target_pairs={{0,1},{1,0},{2,3},{3,2},{4,5},{5,4},{6,7},{7,6},{8,9},{9,8},{10,11... | collective-permute-start | bytes 6152 | tf_op jit(solution)/shard_map/ppermute | solution.py:15
  46.7 1.7 copy-start.8
  46.8 1.9 copy-start.6
  46.8 2.2 copy-start.4
  46.8 3.0 %copy-start.17 = (bf16[256,2,360]{0,2,1:T(8,128)(2,1)}, bf16[256,2,360]{0,2,1:T(8,128)(2,1)S(1)}, u32[]{:S(2)}) copy-start(bf16[256,2,360]{0,2,1:T(8,128)(2,1)S(1)} %get-tuple-element.117) | copy-start | bytes 1105924
  74.8 1.8 copy-start.16
  76.9 4.4 %collective-permute-start.9 = (bf16[256,1,360]{0,2,1:T(8,128)(2,1)S(1)}, bf16[256,1,360]{0,2,1:T(8,128)(2,1)S(1)}, u32[]{:S(2)}, u32[]{:S(2)}) collective-permute-start(bf16[256,1,360]{0,2,1:T(8,128)(2,1)S(1)} %get-tuple-element.135), channel_id=1, source_target_pairs={{2,0},{4,2},{6,4},{0,6},{3,1},{5,3},{7,5},{1,7},{10,8},{12,10},{14... | collective-permute-start | bytes 552968 | tf_op jit(solution)/shard_map/ppermute | solution.py:18
  76.9 6.7 %collective-permute-start.8 = (bf16[256,1,360]{0,2,1:T(8,128)(2,1)S(1)}, bf16[256,1,360]{0,2,1:T(8,128)(2,1)S(1)}, u32[]{:S(2)}, u32[]{:S(2)}) collective-permute-start(bf16[256,1,360]{0,2,1:T(8,128)(2,1)S(1)} %get-tuple-element.134), channel_id=1, source_target_pairs={{0,2},{2,4},{4,6},{6,0},{1,3},{3,5},{5,7},{7,1},{8,10},{10,12},{12... | collective-permute-start | bytes 552968 | tf_op jit(solution)/shard_map/ppermute | solution.py:15
  80.1 7.2 %copy-start.14 = (f32[9,256,256]{2,1,0:T(8,128)}, f32[9,256,256]{2,1,0:T(8,128)S(1)}, u32[]{:S(2)}) copy-start(f32[9,256,256]{2,1,0:T(8,128)S(1)} %fusion.9) | copy-start | bytes 7077892
  83.7 3.7 %collective-permute-start.11 = (bf16[256,4,1]{0,2,1:T(2,128)(2,1)S(1)}, bf16[256,4,1]{0,2,1:T(2,128)(2,1)S(1)}, u32[]{:S(2)}, u32[]{:S(2)}) collective-permute-start(bf16[256,4,1]{0,2,1:T(2,128)(2,1)S(1)} %get-tuple-element.127), channel_id=1, source_target_pairs={{1,0},{0,1},{3,2},{2,3},{5,4},{4,5},{7,6},{6,7},{9,8},{8,9},{11,10... | collective-permute-start | bytes 6152 | tf_op jit(solution)/shard_map/ppermute | solution.py:18
  83.8 3.7 %collective-permute-start.10 = (bf16[256,4,1]{0,2,1:T(2,128)(2,1)S(1)}, bf16[256,4,1]{0,2,1:T(2,128)(2,1)S(1)}, u32[]{:S(2)}, u32[]{:S(2)}) collective-permute-start(bf16[256,4,1]{0,2,1:T(2,128)(2,1)S(1)} %get-tuple-element.126), channel_id=1, source_target_pairs={{0,1},{1,0},{2,3},{3,2},{4,5},{5,4},{6,7},{7,6},{8,9},{9,8},{10,11... | collective-permute-start | bytes 6152 | tf_op jit(solution)/shard_map/ppermute | solution.py:15
  237.0 5.1 %copy-start.1 = (f32[9,256,256]{2,1,0:T(8,128)S(1)}, f32[9,256,256]{2,1,0:T(8,128)}, u32[]{:S(2)}) copy-start(f32[9,256,256]{2,1,0:T(8,128)} %get-tuple-element.104) | copy-start | bytes 7077892
  244.0 1.6 copy-start.39
  (26 other events, 32.0 us)
Sparse Core Ops, SparseCore 0:
  95.2 141.7 all-reduce.3
where the time goes:
time: 256 us
  waiting for transfers between devices  119 us (46%)
  blocking collectives  57.6 us (22%)
  other arithmetic  20.7 us (8%)
  between operations  19.6 us (8%)
  matrix products  18.4 us (7%)
  starting transfers between devices  10.4 us (4%)
  local copies, waits for them, and re-layouts  9.45 us (4%)
    psum x1, waiting for transfers between devices, body(): lax.psum((grad_in, grad_mid, grad_out, grad_noise, loss_term), ('member',...  98.4 us
    psum x1, blocking collectives, body(): lax.psum((grad_in, grad_mid, grad_out, grad_noise, loss_term), ('member',...  40.8 us
    all_gather x1, blocking collectives, body(): lax.all_gather(output[None], 'member', axis=0, tiled=True)  16.8 us
    ppermute x6, waiting for transfers between devices, with_halo(): lax.ppermute(lax.slice_in_dim(block, 0, width, axis=dim), axis, backward)  12.8 us
    ppermute x6, waiting for transfers between devices, with_halo(): lax.ppermute(lax.slice_in_dim(block, block.shape[dim] - width, None, axis...  8.29 us
    dot_general x18, matrix products, conv_forward(): lax.dot_general(weights[offset], window, (((0,), (0,)), ((), ())), prefer...  6.96 us
    ppermute x6, starting transfers between devices, with_halo(): lax.ppermute(lax.slice_in_dim(block, 0, width, axis=dim), axis, backward)  6.79 us
  transfers between devices with their start and end apart: 13, of which 12 were waited for; matrix products, arithmetic and copies ran while one was open for 3% of the time, Pallas kernels for 0%

commit v1 on v0

--- a/solution.py
+++ b/solution.py
@@ -1,23 +1,250 @@
 import jax
 import jax.numpy as jnp
 from jax import lax
+from jax.experimental import pallas as pl
+from jax.experimental.pallas import tpu as pltpu
 from jax.sharding import PartitionSpec as P
 
 SMOOTH = 0.25
 
 
-def with_halo(block, sides, width):
-    for axis, dim in sides:
-        count = lax.axis_size(axis)
-        forward = [(i, i + 1) for i in range(count - 1)]
-        forward.append((count - 1, 0))
-        backward = [(target, source) for source, target in forward]
-        low = lax.ppermute(
-            lax.slice_in_dim(block, block.shape[dim] - width, None, axis=dim), axis, forward
-        )
-        high = lax.ppermute(lax.slice_in_dim(block, 0, width, axis=dim), axis, backward)
-        block = jnp.concatenate([low, block, high], axis=dim)
-    return block
+MESH = pl.DeviceIdType.MESH
+BLOCK = 8
+
+
+def exchange(arrays, routes, cid):
+    sent = len(routes)
+
+    def kernel(*refs):
+        ins = refs[: len(arrays)]
+        outs = refs[len(arrays) : len(arrays) + sent]
+        send_sem, recv_sem = refs[-2:]
+        targets = []
+        for _, shift in routes:
+            targets.append(
+                {
+                    axis: lax.rem(lax.axis_index(axis) + by + lax.axis_size(axis), lax.axis_size(axis))
+                    for axis, by in shift.items()
+                }
+            )
+        barrier = pltpu.get_barrier_semaphore()
+        for target in targets:
+            pl.semaphore_signal(barrier, inc=1, device_id=target, device_id_type=MESH)
+        pl.semaphore_wait(barrier, sent)
+        copies = []
+        for i, (k, _) in enumerate(routes):
+            copy = pltpu.make_async_remote_copy(
+                src_ref=ins[k],
+                dst_ref=outs[i],
+                send_sem=send_sem.at[i],
+                recv_sem=recv_sem.at[i],
+                device_id=targets[i],
+                device_id_type=MESH,
+            )
+            copy.start()
+            copies.append(copy)
+        for copy in copies:
+            copy.wait()
+
+    vmem = pl.BlockSpec(memory_space=pltpu.VMEM)
+    return pl.pallas_call(
+        kernel,
+        out_shape=[jax.ShapeDtypeStruct(arrays[k].shape, arrays[k].dtype) for k, _ in routes],
+        in_specs=[vmem] * len(arrays),
+        out_specs=[vmem] * sent,
+        scratch_shapes=[pltpu.SemaphoreType.DMA((sent,)), pltpu.SemaphoreType.DMA((sent,))],
+        compiler_params=pltpu.CompilerParams(collective_id=cid, has_side_effects=True),
+        name=f"exchange_{cid}",
+    )(*arrays)
+
+
+def with_halo(block, cid):
+    rows = block.shape[1]
+    arrays = [block[:, rows - 1], block[:, 0], block[:, :, -1].T, block[:, :, 0].T]
+    routes = [
+        (0, {"lat": 1}),
+        (1, {"lat": -1}),
+        (2, {"lon": 1}),
+        (3, {"lon": -1}),
+        (2, {"lat": 1, "lon": 1}),
+        (3, {"lat": 1, "lon": -1}),
+        (2, {"lat": -1, "lon": 1}),
+        (3, {"lat": -1, "lon": -1}),
+    ]
+    above, below, left, right, above_left, above_right, below_left, below_right = exchange(
+        arrays, routes, cid
+    )
+    low = jnp.concatenate([above_left[rows - 1 :], left, below_left[:1]], axis=0).T
+    high = jnp.concatenate([above_right[rows - 1 :], right, below_right[:1]], axis=0).T
+    middle = jnp.concatenate([above[:, None], block, below[:, None]], axis=1)
+    return jnp.concatenate([low[:, :, None], middle, high[:, :, None]], axis=2)
+
+
+def reduce_groups():
+    lat, lats = lax.axis_index("lat"), lax.axis_size("lat")
+    cores = 2 if lats % 2 == 0 else 1
+    core, row = lax.rem(lat, cores), lat // cores
+    return {
+        "core": (cores, core, lambda p: {"lat": row * cores + p}),
+        "row": (lats // cores, row, lambda p: {"lat": p * cores + core}),
+        "lon": (lax.axis_size("lon"), lax.axis_index("lon"), lambda p: {"lon": p}),
+        "member": (lax.axis_size("member"), lax.axis_index("member"), lambda p: {"member": p}),
+    }
+
+
+ORDERS = (("core", "row", "lon", "member"), ("core", "lon", "row", "member"), ("core", "member", "row", "lon"))
+
+
+def split_units(units):
+    last = units // 7
+    first = (units - last + 1) // 2
+    return (first, units - last - first, last)
+
+
+def sum_everywhere(array, cid):
+    devices = lax.axis_size("lat") * lax.axis_size("lon") * lax.axis_size("member")
+    rows = array.shape[0]
+    unit = BLOCK * devices
+    spans = []
+    base = 0
+    for order, units in zip(ORDERS, split_units(rows // unit)):
+        if units:
+            spans.append((order, base, units * unit))
+            base += units * unit
+    sizes = {
+        "core": 2 if lax.axis_size("lat") % 2 == 0 else 1,
+        "lon": lax.axis_size("lon"),
+        "member": lax.axis_size("member"),
+    }
+    sizes["row"] = lax.axis_size("lat") // sizes["core"]
+    plans = []
+    landing = 0
+    flags = 0
+    for order, base, span in spans:
+        steps = []
+        for name in order:
+            n = sizes[name]
+            span //= n
+            steps.append((name, n, span, landing, flags))
+            landing += (n - 1) * span
+            flags += n - 1
+        plans.append((base, steps))
+    stages = len(ORDERS[0])
+
+    def kernel(in_ref, out_ref, held, landed, send_sem, recv_sem, send_back, recv_back):
+        groups = reduce_groups()
+        barrier = pltpu.get_barrier_semaphore()
+        partners = 0
+        for n, place, device in groups.values():
+            for d in range(1, n):
+                pl.semaphore_signal(
+                    barrier, inc=1, device_id=device(lax.rem(place + d, n)), device_id_type=MESH
+                )
+                partners += 1
+        pl.semaphore_wait(barrier, partners)
+        starts = [[base] for base, _ in plans]
+        for stage in range(stages):
+            source = in_ref if stage == 0 else held
+            target = out_ref if stage == stages - 1 else held
+            running = []
+            for p, (_, steps) in enumerate(plans):
+                name, n, span, land, flag = steps[stage]
+                _, place, device = groups[name]
+                start = starts[p][-1]
+                for d in range(1, n):
+                    other = lax.rem(place + d, n)
+                    copy = pltpu.make_async_remote_copy(
+                        src_ref=source.at[pl.ds(pl.multiple_of(start + other * span, BLOCK), span)],
+                        dst_ref=landed.at[pl.ds(land + (d - 1) * span, span)],
+                        send_sem=send_sem.at[flag + d - 1],
+                        recv_sem=recv_sem.at[flag + d - 1],
+                        device_id=device(other),
+                        device_id_type=MESH,
+                    )
+                    copy.start()
+                    running.append((p, copy))
+            for p, (_, steps) in enumerate(plans):
+                name, n, span, land, flag = steps[stage]
+                mine = starts[p][-1] + groups[name][1] * span
+                starts[p].append(mine)
+                for q, copy in running:
+                    if q == p:
+                        copy.wait()
+                chunk = BLOCK
+                while chunk < 64 and span % (2 * chunk) == 0:
+                    chunk *= 2
+
+                def add(i, carry, mine=mine, n=n, span=span, land=land, chunk=chunk):
+                    at = pl.ds(pl.multiple_of(mine + i * chunk, BLOCK), chunk)
+                    total = source[at]
+                    for d in range(1, n):
+                        total = total + landed[
+                            pl.ds(pl.multiple_of(land + (d - 1) * span + i * chunk, BLOCK), chunk)
+                        ]
+                    target[at] = total
+                    return carry
+
+                lax.fori_loop(0, span // chunk, add, 0)
+        for stage in reversed(range(stages)):
+            running = []
+            for p, (_, steps) in enumerate(plans):
+                name, n, span, _, flag = steps[stage]
+                _, place, device = groups[name]
+                at = pl.ds(pl.multiple_of(starts[p][stage + 1], BLOCK), span)
+                for d in range(1, n):
+                    copy = pltpu.make_async_remote_copy(
+                        src_ref=out_ref.at[at],
+                        dst_ref=out_ref.at[at],
+                        send_sem=send_back.at[flag + d - 1],
+                        recv_sem=recv_back.at[flag + d - 1],
+                        device_id=device(lax.rem(place + d, n)),
+                        device_id_type=MESH,
+                    )
+                    copy.start()
+                    running.append(copy)
+            for copy in running:
+                copy.wait()
+
+    vmem = pl.BlockSpec(memory_space=pltpu.VMEM)
+    dma = pltpu.SemaphoreType.DMA((flags,))
+    return pl.pallas_call(
+        kernel,
+        out_shape=jax.ShapeDtypeStruct(array.shape, array.dtype),
+        in_specs=[vmem],
+        out_specs=vmem,
+        scratch_shapes=[
+            pltpu.VMEM(array.shape, array.dtype),
+            pltpu.VMEM((landing, array.shape[1]), array.dtype),
+            dma,
+            dma,
+            dma,
+            dma,
+        ],
+        compiler_params=pltpu.CompilerParams(collective_id=cid, has_side_effects=True),
+        name="sum_everywhere",
+    )(array)
+
+
+def sum_gradients(grad_in, grad_mid, grad_out, grad_noise, loss_term):
+    devices = lax.axis_size("lat") * lax.axis_size("lon") * lax.axis_size("member")
+    width = grad_in.shape[-1]
+    parts = []
+    places = []
+    rows = 0
+    for value in (grad_in, grad_mid, grad_out, grad_noise, jnp.full((1, width), loss_term)):
+        short = -value.shape[-2] % BLOCK
+        padded = jnp.pad(value, ((0, 0),) * (value.ndim - 2) + ((0, short), (0, 0)))
+        flat = padded.reshape(-1, width)
+        parts.append(flat)
+        places.append((rows, flat.shape[0], padded.shape, value.shape[-2]))
+        rows += flat.shape[0]
+    parts.append(jnp.zeros((-rows % (BLOCK * devices), width), jnp.float32))
+    summed = sum_everywhere(jnp.concatenate(parts, axis=0), 5)
+    back = [
+        summed[start : start + count].reshape(shape)[..., :real, :]
+        for start, count, shape, real in places
+    ]
+    return (*back[:4], back[4][0, 0])
 
 
 def shifted(padded, offset, row_count, col_count):
@@ -81,14 +308,13 @@
 
 
 def pair_sums(outputs, others, running):
-
-    def add_member(totals, member_out):
+    slopes, spreads = running
+    for member_out in others:
         gap_value = outputs - member_out.astype(jnp.float32)[None]
         radius = jnp.sqrt(gap_value * gap_value + SMOOTH * SMOOTH)
-        return ((totals[0] + gap_value / radius, totals[1] + radius - SMOOTH), None)
-
-    sums, _ = lax.scan(add_member, running, others)
-    return sums
+        slopes = slopes + gap_value / radius
+        spreads = spreads + (radius - SMOOTH)
+    return slopes, spreads
 
 
 def normalize(gradient):
@@ -104,14 +330,12 @@
     members = lax.axis_size("member")
     latent = (seeds[0].astype(jnp.float32) - 32767.5) / 18918.0
     noise_bias = jnp.dot(latent, w_noise, precision=lax.Precision.HIGHEST)
-    state_pad = with_halo(state, (("lat", 1), ("lon", 2)), 1)
+    state_pad = with_halo(state, 1)
     state_pad = clear_outside(state_pad, 1, lat_index, lat_count)
     pre_in = conv_forward(w_in, state_pad, row_count, col_count) + noise_bias[:, None]
     act_in, slope_in = gelu_pair(pre_in)
     hidden_in = act_in.astype(jnp.bfloat16)
-    hidden_pad = with_halo(
-        hidden_in.reshape(channels, row_count, col_count), (("lat", 1), ("lon", 2)), 1
-    )
+    hidden_pad = with_halo(hidden_in.reshape(channels, row_count, col_count), 2)
     hidden_pad = clear_outside(hidden_pad, 1, lat_index, lat_count)
     pre_mid = conv_forward(w_mid, hidden_pad, row_count, col_count)
     act_mid, slope_mid = gelu_pair(pre_mid)
@@ -124,9 +348,8 @@
     weights = 1.0 + land_sea.reshape(1, cell_count).astype(jnp.float32)
     own_output = output.astype(jnp.float32)[None]
     blank = jnp.zeros(own_output.shape, jnp.float32)
-    slope_sum, spread_sum = pair_sums(
-        own_output, lax.all_gather(output[None], "member", axis=0, tiled=True), (blank, blank)
-    )
+    others = exchange([output], [(0, {"member": d}) for d in range(1, members)], 4)
+    slope_sum, spread_sum = pair_sums(own_output, [output, *others], (blank, blank))
     gradients, loss_term = combine(own_output, target_flat, weights, slope_sum, spread_sum, members)
     delta_out = gradients[0].astype(jnp.bfloat16)
     grad_out = lax.dot_general(
@@ -136,17 +359,15 @@
         w_out, delta_out, (((0,), (0,)), ((), ())), preferred_element_type=jnp.float32
     )
     delta_mid = (upstream * slope_mid).astype(jnp.bfloat16)
-    delta_pad = with_halo(
-        delta_mid.reshape(channels, row_count, col_count), (("lat", 1), ("lon", 2)), 1
-    )
+    delta_pad = with_halo(delta_mid.reshape(channels, row_count, col_count), 3)
     delta_pad = clear_outside(delta_pad, 1, lat_index, lat_count)
     incoming = conv_back(w_mid, delta_pad, row_count, col_count) + upstream
     delta_in = (incoming * slope_in).astype(jnp.bfloat16)
     grad_mid = weight_grad(hidden_pad, delta_mid, row_count, col_count)
     grad_in = weight_grad(state_pad, delta_in, row_count, col_count)
     grad_noise = latent[:, None] * jnp.sum(delta_in.astype(jnp.float32), axis=1)[None, :]
-    grad_in, grad_mid, grad_out, grad_noise, summed = lax.psum(
-        (grad_in, grad_mid, grad_out, grad_noise, loss_term), ("member", "lat", "lon")
+    grad_in, grad_mid, grad_out, grad_noise, summed = sum_gradients(
+        grad_in, grad_mid, grad_out, grad_noise, loss_term
     )
     loss = summed / (variables * cell_count * lat_count * lax.axis_size("lon"))
     return (

time: 256 us -> 214 us (0.84); the launches traced: 256 us -> 210 us
  waiting for transfers between devices: 119 us -> 0 us
  Pallas kernels: 0 us -> 110 us
  blocking collectives: 57.6 us -> 0 us
  local copies, waits for them, and re-layouts: 9.45 us -> 37.5 us
  matrix products: 18.4 us -> 33.6 us
  between operations: 19.6 us -> 6.07 us
  starting transfers between devices: 10.4 us -> 0 us
  other arithmetic: 20.7 us -> 23.5 us
    pallas_call x0 -> x5, Pallas kernels: none -> 110 us  [the longest x1 65.5 us: sum_everywhere(): pl.pallas_call(kernel, out_shape=jax.ShapeDtypeStruct(array.shape, array....]
    psum x1 -> x0, waiting for transfers between devices: 98.4 us -> none  [body(): lax.psum((grad_in, grad_mid, grad_out, grad_noise, loss_term), ('member',...]
    psum x1 -> x0, blocking collectives: 40.8 us -> none  [body(): lax.psum((grad_in, grad_mid, grad_out, grad_noise, loss_term), ('member',...]
    ppermute x12 -> x0, waiting for transfers between devices: 21 us -> none  [the longest x6 12.8 us: with_halo(): lax.ppermute(lax.slice_in_dim(block, 0, width, axis=dim), axis, backward)]
    all_gather x1 -> x0, blocking collectives: 16.8 us -> none  [body(): lax.all_gather(output[None], 'member', axis=0, tiled=True)]
    ppermute x12 -> x0, starting transfers between devices: 10.4 us -> none  [the longest x6 6.79 us: with_halo(): lax.ppermute(lax.slice_in_dim(block, 0, width, axis=dim), axis, backward)]
    unnamed x90 -> x88, local copies, waits for them, and re-layouts: 2.83 us -> 11.3 us
    dot_general x18, matrix products: 6.96 us -> 14.7 us  [conv_forward(): lax.dot_general(weights[offset], window, (((0,), (0,)), ((), ())), prefer...]
  transfers between devices with their start and end apart: 13 -> 0, of which waited for: 12 -> 0; matrix products, arithmetic and copies ran while one was open for 3% -> 0% of each run, Pallas kernels for 0% -> 0%
where the time goes in v1:
time: 214 us; the launch traced here: 210 us
  Pallas kernels  110 us (51%)
  local copies, waits for them, and re-layouts  37.5 us (18%)
  matrix products  33.6 us (16%)
  other arithmetic  23.5 us (11%)
  between operations  6.07 us (3%)
    pallas_call x1, Pallas kernels, sum_everywhere(): pl.pallas_call(kernel, out_shape=jax.ShapeDtypeStruct(array.shape, array....  65.5 us
    pallas_call x4, Pallas kernels, exchange(): pl.pallas_call(kernel, out_shape=[jax.ShapeDtypeStruct(arrays[k].shape, a...  44.3 us
    dot_general x18, matrix products, conv_forward(): lax.dot_general(weights[offset], window, (((0,), (0,)), ((), ())), prefer...  14.7 us
    unnamed x88, local copies, waits for them, and re-layouts  11.3 us
    dot_general x18, matrix products, weight_grad(): lax.dot_general(window, deltas, (((1,), (1,)), ((), ())), preferred_eleme...  10.9 us
    div x4, other arithmetic, normalize(): return gradient / jnp.sqrt(jnp.mean(gradient * gradient) + 1e-06)  7.17 us
    reduce_sum x4, other arithmetic, normalize(): return gradient / jnp.sqrt(jnp.mean(gradient * gradient) + 1e-06)  6.62 us

profile of v1, /device:TPU:0, one launch (start us, length us, event | category | flops | bytes accessed | tf_op | source)
XLA Modules:
  0.0 210.4 jit_solution(3548978480518755217)
XLA Ops:
  0.7 1.3 fusion.132
  4.9 8.4 %exchange_1.1 = (bf16[100,360]{1,0:T(8,128)(2,1)}, bf16[100,360]{1,0:T(8,128)(2,1)}, bf16[2,100]{1,0:T(2,128)(2,1)}, bf16[2,100]{1,0:T(2,128)(2,1)}, bf16[2,100]...) custom-call(bf16[100,360]{1,0:T(8,128)(2,1)} %get-tuple-element.109.refs_0_, ...), custom_call_target="tpu_custom_call" | custom-call | tf_op jit(solution)/shard_map/exchange_1/pallas_call | solution.py:50
  18.3 1.3 maximum_select_fusion.2
  19.6 1.4 fusion.130
  21.2 1.1 fusion.110
  22.5 1.1 convolution_add_fusion.23
  23.8 1.1 convolution_add_fusion.22
  25.1 1.1 convolution_add_fusion.21
  26.5 1.1 convolution_add_fusion.20
  27.8 1.1 convolution_add_fusion.19
  29.1 1.1 convolution_add_fusion.18
  30.5 1.1 convolution_add_fusion.17
  31.9 2.1 %multiply_convert_fusion = (bf16[256,720]{0,1:T(8,128)(2,1)S(1)}, f32[256,720]{0,1:T(8,128)}) fusion(f32[256]{0:T(256)S(1)} %bitcast.399, f32[720,256]{1,0:T(8,128)S(1)} %convolution_add_fusion.17, bf16[100,720]{1,0:T(8,128)(2,1)S(1)} %reshape.228, bf16[9,100,256]{2,1,0:T(8,128)(2,1)} %param.12), kind=kOutput, calls=%fused_computation.105 | convolution fusion | flops 38891520 | bytes 2041472 | tf_op jit(solution)/shard_map/dot_general | solution.py:261
  36.9 9.2 %exchange_2.1 = (bf16[256,360]{1,0:T(8,128)(2,1)}, bf16[256,360]{1,0:T(8,128)(2,1)}, bf16[2,256]{1,0:T(2,128)(2,1)}, bf16[2,256]{1,0:T(2,128)(2,1)}, bf16[2,256]...) custom-call(bf16[256,360]{1,0:T(8,128)(2,1)} %copy.39.refs_0_, ...), custom_call_target="tpu_custom_call" | custom-call | tf_op jit(solution)/shard_map/exchange_2/pallas_call | solution.py:50
  48.5 1.1 copy.42
  55.2 1.4 add_convert_fusion
  57.5 2.0 fusion.17.refs_0_
  59.5 17.1 %exchange_4.1 = (bf16[100,720]{1,0:T(8,128)(2,1)}, bf16[100,720]{1,0:T(8,128)(2,1)}, bf16[100,720]{1,0:T(8,128)(2,1)}) custom-call(bf16[100,720]{1,0:T(8,128)(2,1)} %fusion.17.refs_0_), custom_call_target="tpu_custom_call" | custom-call | tf_op jit(solution)/shard_map/exchange_4/pallas_call | solution.py:50
  77.8 2.8 %fusion.63 = (f32[]{:T(128)}, bf16[100,720]{1,0:T(8,128)(2,1)S(1)}) fusion(bf16[100,720]{1,0:T(8,128)(2,1)} %get-tuple-element.50, bf16[100,720]{1,0:T(8,128)(2,1)} %get-tuple-element.49, bf16[100,720]{1,0:T(8,128)(2,1)} %get-tuple-element.48, bf16[100,720]{1,0:T(8,128)(2,1)} %fusion.17.refs_0_, f32[100,720]{1,0:T(8,128)S(1)} %reshape.253, f32[720]{0:T(1024)S(1)} %add.237), kind=kLoop, calls=%fused_computation.130 | loop fusion | flops 3239999 | bytes 1010884 | tf_op jit(solution)/shard_map/reduce_sum | solution.py:304
  80.6 2.6 %fusion.48 = (bf16[256,720]{0,1:T(8,128)(2,1)S(1)}, f32[256,720]{0,1:T(8,128)}) fusion(f32[256,720]{0,1:T(8,128)} %get-tuple-element.103, bf16[100,720]{1,0:T(8,128)(2,1)S(1)} %get-tuple-element.60, bf16[100,256]{1,0:T(8,128)(2,1)S(1)} %copy-done), kind=kOutput, calls=%fused_computation.102 | convolution fusion | flops 40181760 | bytes 2038400 | tf_op jit(solution)/shard_map/dot_general | solution.py:358
  95.0 9.6 %exchange_3.1 = (bf16[256,360]{1,0:T(8,128)(2,1)}, bf16[256,360]{1,0:T(8,128)(2,1)}, bf16[2,256]{1,0:T(2,128)(2,1)}, bf16[2,256]{1,0:T(2,128)(2,1)}, bf16[2,256]...) custom-call(bf16[256,360]{1,0:T(8,128)(2,1)} %copy.47.refs_0_, ...), custom_call_target="tpu_custom_call" | custom-call | tf_op jit(solution)/shard_map/exchange_3/pallas_call | solution.py:50
  107.1 1.1 copy.50
  117.3 3.3 %constant_dynamic-update-slice_fusion.2 = f32[3584,256]{1,0:T(8,128)} fusion(f32[3584,256]{1,0:T(8,128)} %constant_dynamic-update-slice_fusion.3, f32[2304,256]{1,0:T(8,128)} %bitcast.101), kind=kLoop, calls=%fused_computation.201 | loop fusion | bytes 4718592
  124.1 65.5 %sum_everywhere.1 = f32[3584,256]{1,0:T(8,128)} custom-call(f32[3584,256]{1,0:T(8,128)} %broadcast_dynamic-update-slice_fusion.in_ref), custom_call_target="tpu_custom_call" | custom-call | tf_op jit(solution)/shard_map/sum_everywhere/pallas_call | solution.py:210
  189.6 1.4 multiply_reduce_fusion.3
  191.6 1.4 slice_divide_fusion.3
  193.0 1.5 multiply_reduce_fusion.2
  195.2 1.6 slice_divide_fusion.2
  196.8 2.9 %multiply_reduce_fusion = f32[]{:T(128)} fusion(f32[3584,256]{1,0:T(8,128)} %sum_everywhere.1), kind=kLoop, calls=%fused_computation | loop fusion | flops 1179647 | bytes 2359300 | tf_op jit(solution)/shard_map/reduce_sum | solution.py:321
  200.4 3.2 %slice_divide_fusion = f32[2304,256]{1,0:T(8,128)} fusion(f32[3584,256]{1,0:T(8,128)} %sum_everywhere.1, f32[]{:T(128)S(6)} %sqrt.38), kind=kLoop, calls=%fused_computation.1 | loop fusion | flops 589824 | bytes 4718596 | tf_op jit(solution)/shard_map/div | solution.py:321
  203.6 1.3 slice.327
  207.4 1.2 slice.332
  (181 shorter events, 50.6 us)
Async XLA Ops:
  0.6 56.9 %copy-start = (bf16[100,256]{1,0:T(8,128)(2,1)S(1)}, bf16[100,256]{1,0:T(8,128)(2,1)}, u32[]{:S(2)}) copy-start(bf16[100,256]{1,0:T(8,128)(2,1)} %param.14) | copy-start | bytes 153604
  0.6 17.6 %copy-start.2 = (bf16[100,2,360]{2,1,0:T(2,128)(2,1)S(1)}, bf16[100,2,360]{2,1,0:T(2,128)(2,1)}, u32[]{:S(2)}) copy-start(bf16[100,2,360]{2,1,0:T(2,128)(2,1)} %param.8) | copy-start | bytes 432004
  22.5 3.8 %copy-start.14 = (bf16[100,720]{1,0:T(8,128)(2,1)}, bf16[100,720]{1,0:T(8,128)(2,1)S(1)}, u32[]{:S(2)}) copy-start(bf16[100,720]{1,0:T(8,128)(2,1)S(1)} %reshape.221) | copy-start | bytes 432004
  23.8 3.8 %copy-start.16 = (bf16[100,720]{1,0:T(8,128)(2,1)}, bf16[100,720]{1,0:T(8,128)(2,1)S(1)}, u32[]{:S(2)}) copy-start(bf16[100,720]{1,0:T(8,128)(2,1)S(1)} %reshape.222) | copy-start | bytes 432004
  25.1 3.8 %copy-start.18 = (bf16[100,720]{1,0:T(8,128)(2,1)}, bf16[100,720]{1,0:T(8,128)(2,1)S(1)}, u32[]{:S(2)}) copy-start(bf16[100,720]{1,0:T(8,128)(2,1)S(1)} %reshape.223) | copy-start | bytes 432004
  26.4 3.8 %copy-start.20 = (bf16[100,720]{1,0:T(8,128)(2,1)}, bf16[100,720]{1,0:T(8,128)(2,1)S(1)}, u32[]{:S(2)}) copy-start(bf16[100,720]{1,0:T(8,128)(2,1)S(1)} %reshape.224) | copy-start | bytes 432004
  27.8 3.8 %copy-start.22 = (bf16[100,720]{1,0:T(8,128)(2,1)}, bf16[100,720]{1,0:T(8,128)(2,1)S(1)}, u32[]{:S(2)}) copy-start(bf16[100,720]{1,0:T(8,128)(2,1)S(1)} %reshape.225) | copy-start | bytes 432004
  28.9 2.8 %copy-start.34 = (f32[32,256]{1,0:T(8,128)S(1)}, f32[32,256]{1,0:T(8,128)}, u32[]{:S(2)}) copy-start(f32[32,256]{1,0:T(8,128)} %param.15) | copy-start | bytes 98308
  29.0 2.8 %copy-start.36 = (s32[1,32]{1,0:T(1,128)S(1)}, s32[1,32]{1,0:T(1,128)}, u32[]{:S(2)}) copy-start(s32[1,32]{1,0:T(1,128)} %param.11) | copy-start | bytes 388
  29.1 5.0 %copy-start.24 = (bf16[100,720]{1,0:T(8,128)(2,1)}, bf16[100,720]{1,0:T(8,128)(2,1)S(1)}, u32[]{:S(2)}) copy-start(bf16[100,720]{1,0:T(8,128)(2,1)S(1)} %reshape.226) | copy-start | bytes 432004
  30.5 3.7 %copy-start.26 = (bf16[100,720]{1,0:T(8,128)(2,1)}, bf16[100,720]{1,0:T(8,128)(2,1)S(1)}, u32[]{:S(2)}) copy-start(bf16[100,720]{1,0:T(8,128)(2,1)S(1)} %reshape.227) | copy-start | bytes 432004
  31.8 17.8 %copy-start.30 = (bf16[100,720]{1,0:T(8,128)(2,1)}, bf16[100,720]{1,0:T(8,128)(2,1)S(1)}, u32[]{:S(2)}) copy-start(bf16[100,720]{1,0:T(8,128)(2,1)S(1)} %reshape.228) | copy-start | bytes 432004
  34.1 16.9 %copy-start.7 = (bf16[256,720]{0,1:T(8,128)(2,1)}, bf16[256,720]{0,1:T(8,128)(2,1)S(1)}, u32[]{:S(2)}) copy-start(bf16[256,720]{0,1:T(8,128)(2,1)S(1)} %get-tuple-element.100) | copy-start | bytes 1105924
  51.7 1.7 copy-start.3
  51.7 1.7 copy-start.5
  51.8 1.7 copy-start.10
  51.8 3.0 %copy-start.12 = (bf16[256,2,360]{0,2,1:T(8,128)(2,1)}, bf16[256,2,360]{0,2,1:T(8,128)(2,1)S(1)}, u32[]{:S(2)}) copy-start(bf16[256,2,360]{0,2,1:T(8,128)(2,1)S(1)} %get-tuple-element.70) | copy-start | bytes 1105924
  55.2 22.5 %copy-start.35 = (s32[2,360]{1,0:T(2,128)S(1)}, s32[2,360]{1,0:T(2,128)}, u32[]{:S(2)}) copy-start(s32[2,360]{1,0:T(2,128)} %param.10) | copy-start | bytes 8644
  80.6 3.6 %copy-start.32 = (bf16[100,720]{1,0:T(8,128)(2,1)}, bf16[100,720]{1,0:T(8,128)(2,1)S(1)}, u32[]{:S(2)}) copy-start(bf16[100,720]{1,0:T(8,128)(2,1)S(1)} %get-tuple-element.60) | copy-start | bytes 432004
  80.6 2.6 %copy-start.11 = (bf16[256,2,360]{0,2,1:T(8,128)(2,1)S(1)}, bf16[256,2,360]{0,2,1:T(8,128)(2,1)}, u32[]{:S(2)}) copy-start(bf16[256,2,360]{0,2,1:T(8,128)(2,1)} %copy-done.10) | copy-start | bytes 1105924
  80.6 3.6 %copy-start.6 = (bf16[256,2,360]{0,2,1:T(8,128)(2,1)S(1)}, bf16[256,2,360]{0,2,1:T(8,128)(2,1)}, u32[]{:S(2)}) copy-start(bf16[256,2,360]{0,2,1:T(8,128)(2,1)} %copy-done.5) | copy-start | bytes 1105924
  80.6 4.6 %copy-start.4 = (bf16[256,2,360]{0,2,1:T(8,128)(2,1)S(1)}, bf16[256,2,360]{0,2,1:T(8,128)(2,1)}, u32[]{:S(2)}) copy-start(bf16[256,2,360]{0,2,1:T(8,128)(2,1)} %copy-done.3) | copy-start | bytes 1105924
  86.2 5.0 %copy-start.13 = (bf16[256,2,360]{0,2,1:T(8,128)(2,1)S(1)}, bf16[256,2,360]{0,2,1:T(8,128)(2,1)}, u32[]{:S(2)}) copy-start(bf16[256,2,360]{0,2,1:T(8,128)(2,1)} %copy-done.12) | copy-start | bytes 1105924
  112.1 1.3 copy-start.38
  112.7 1.4 copy-start.29
  113.4 1.4 copy-start.19
  113.4 1.6 copy-start.21
  114.1 1.4 copy-start.25
  114.1 1.6 copy-start.27
  114.3 1.6 copy-start.31
  117.3 3.3 %copy-start.9 = (bf16[256,720]{0,1:T(8,128)(2,1)S(1)}, bf16[256,720]{0,1:T(8,128)(2,1)}, u32[]{:S(2)}) copy-start(bf16[256,720]{0,1:T(8,128)(2,1)} %get-tuple-element.102) | copy-start | bytes 1105924
  117.3 3.3 %copy-start.33 = (bf16[100,720]{1,0:T(8,128)(2,1)S(1)}, bf16[100,720]{1,0:T(8,128)(2,1)}, u32[]{:S(2)}) copy-start(bf16[100,720]{1,0:T(8,128)(2,1)} %copy-done.32) | copy-start | bytes 432004
  (7 other events, 7.8 us)
